TPU v7x, 16 devices: a whole 2x2x2 slice. The times are simulated.
16 devices in a mesh: tp: 2 (over z), dp: 8 (over y, x, core).
Axes of the slice: x: 2, y: 2, z: 2, core: 2. Of those that a mesh axis runs over, the one named last changes fastest.
Arguments:
- hidden: bfloat16 [8192, 2048], P('dp')
- embedding: bfloat16 [49152, 2048], P('tp')
- norm_weight: float32 [2048], replicated
- teach_ids: int32 [8192, 256], P('dp')
- teach_prob: float32 [8192, 256], P('dp')
- tok_mask: float32 [8192], P('dp')
Outputs:
- output 1: float32 [], replicated
- output 2: bfloat16 [8192, 2048], P('dp')
- output 3: float32 [49152, 2048], P('tp', 'dp')
- output 4: float32 [2048], replicated
All inputs are finite; a program needn't handle non-finite values.
Results may differ from a plain program's by a relative error of at most 0.001.
Values sent between devices are 32-bit elements.
A program may use at most 1 GiB of HBM per device.

v0:
```python
import jax
import jax.numpy as jnp
from jax import lax
from jax.sharding import PartitionSpec as P

EPS_NORM = 1e-6


def solution(mesh):
    def local_head(hidden, embedding, norm_weight, teach_ids, teach_prob, tok_mask):
        vocab_local = embedding.shape[0]
        tok_local = hidden.shape[0]
        shard_pos = lax.axis_index('tp')
        mask_total = lax.psum(jnp.sum(tok_mask), 'dp')
        scale_w = 1.0 + norm_weight
        h_f32 = hidden.astype(jnp.float32)
        inv_rms = lax.rsqrt(jnp.mean(h_f32 * h_f32, axis=1, keepdims=True) + EPS_NORM)
        normed = h_f32 * inv_rms
        normed_bf = (normed * scale_w).astype(jnp.bfloat16)
        logits = lax.dot_general(normed_bf, embedding, (((1,), (1,)), ((), ())), preferred_element_type=jnp.float32)
        row_max = lax.pmax(jnp.max(logits, axis=1, keepdims=True), 'tp')
        shifted = jnp.exp(logits - row_max)
        local_ids = teach_ids - shard_pos * vocab_local
        in_range = (local_ids >= 0) & (local_ids < vocab_local)
        safe_ids = jnp.where(in_range, local_ids, 0)
        picked = jnp.take_along_axis(logits, safe_ids, axis=1)
        teach_part = jnp.sum(jnp.where(in_range, teach_prob * picked, 0.0), axis=1)
        row_stats = lax.psum(jnp.stack([jnp.sum(shifted, axis=1), teach_part], axis=1), 'tp')
        sum_exp = row_stats[:, 0:1]
        log_norm = row_max + jnp.log(sum_exp)
        loss_sum = lax.psum(jnp.sum(tok_mask * (row_stats[:, 1] - log_norm[:, 0])), 'dp')
        loss_mean = -loss_sum / mask_total
        weight = (tok_mask / mask_total)[:, None]
        soft_prob = shifted * (1.0 / sum_exp)
        row_ids = jnp.arange(tok_local)[:, None]
        d_logits = (soft_prob * weight).at[row_ids, safe_ids].add(jnp.where(in_range, -teach_prob * weight, 0.0))
        dlogit_bf = d_logits.astype(jnp.bfloat16)
        grad_u = lax.psum(jnp.dot(dlogit_bf, embedding, preferred_element_type=jnp.float32), 'tp')
        embed_part = lax.dot_general(dlogit_bf, normed_bf, (((0,), (0,)), ((), ())), preferred_element_type=jnp.float32)
        grad_embed = lax.psum_scatter(embed_part, 'dp', scatter_dimension=1, tiled=True)
        d_normed = grad_u * scale_w
        grad_hidden = (inv_rms * (d_normed - normed * jnp.mean(d_normed * normed, axis=1, keepdims=True))).astype(jnp.bfloat16)
        grad_norm = lax.psum(jnp.sum(grad_u * normed, axis=0), 'dp')
        return loss_mean, grad_hidden, grad_embed, grad_norm

    return jax.shard_map(local_head, mesh=mesh, in_specs=(P('dp', None), P('tp', None), P(None), P('dp', None), P('dp', None), P('dp')), out_specs=(P(), P('dp', None), P('tp', 'dp'), P(None)), check_vma=False)
```

profile of v0, /device:TPU:0, one launch (start us, length us, event | category | flops | bytes accessed | tf_op | source)
XLA Modules:
  0.0 12505.5 jit_solution(15313830357336938233)
XLA Ops:
  7.2 3.1 fusion.11
  10.3 0.7 broadcast_add_fusion
  11.0 1.7 or_bitcast_fusion
  12.8 1.5 copy.10
  15.2 1.5 copy.12
  16.7 115.1 fusion.19
  131.8 6.8 pmax.7
  138.6 5059.2 %gather_fusion = f32[262144]{0:T(1024)S(1)} fusion(f32[1024,24576]{1,0:T(8,128)} %get-tuple-element.17, s32[262144]{0:T(1024)} %bitcast.28), kind=kCustom, calls=%fused_computation | custom fusion | bytes 4194304 | tf_op jit(solution)/shard_map/jit(take_along_axis)/gather | solution.py:26
  5198.1 31.0 fusion
  5229.8 3861.5 %psum.35 = f32[1024,2]{0,1:T(2,128)S(1)} all-reduce(f32[1024,2]{0,1:T(2,128)S(1)} %pad_maximum_fusion), channel_id=1, replica_groups=mesh['tp'=2,'dp'=8] {'tp'}, use_global_device_ids=true, to_apply=%region_5.6 | all-reduce | flops 2048 | bytes 16384 | tf_op jit(solution)/shard_map/psum | solution.py:28
  9091.9 13.5 psum.37
  9106.4 1.5 copy.13
  9108.0 65.0 multiply_bitcast_fusion
  9173.0 65.6 copy.11
  9238.6 1788.9 %scatter_fusion = f32[25165824]{0:T(1024)} fusion(f32[25165824]{0:T(1024)} %bitcast.11, s32[262144]{0:T(1024)} %get-tuple-element.4, f32[262144]{0:T(1024)} %get-tuple-element.5), kind=kCustom, calls=%fused_computation.1 | custom fusion | flops 262144 | bytes 4194304
  11027.4 47.9 convert_element_type.16
  11075.3 64.0 reshape.39
  11139.4 114.9 fusion.20
  11254.9 119.5 fusion.12
  11374.4 73.2 all-reduce.3.cloned.1.call-done
  11447.6 5.8 fusion.10
  11453.5 14.4 all-reduce
  11469.2 6.9 fusion.9
  11476.1 1021.3 %reduce-scatter.2.cloned.1.call-done = f32[24576,256]{1,0:T(8,128)} async-done(((f32[24576,2048]{1,0:T(8,128)}), f32[24576,256]{1,0:T(8,128)}) %reduce-scatter.2.cloned.1.call-update) | async-done | bytes 25165840 | tf_op jit(solution)/shard_map/reduce_scatter | solution.py:40
  (40 shorter events, 4.2 us)
Async XLA Ops:
  7.2 7.2 copy-start.8
  7.2 7.6 copy-start.9
  7.2 9231.4 %sort.2.cloned.1.call-start = ((), (), s32[]{:S(2)}) async-start(), calls=%async_computation.3 | async-start | bytes 6291488
  10.3 121.5 copy-start.5
  11.0 120.8 copy-start.2
  138.6 5059.5 %copy-start.4 = (f32[1024,1]{0,1:T(1,128)S(1)}, f32[1024,1]{0,1:T(1,128)}, u32[]{:S(2)}) copy-start(f32[1024,1]{0,1:T(1,128)} %pmax.7) | copy-start | bytes 12292
  5198.1 31.1 copy-start
  5198.1 31.1 copy-start.1
  5198.1 3893.2 %copy-start.7 = (f32[1024]{0:T(1024)S(1)}, f32[1024]{0:T(1024)}, u32[]{:S(2)}) copy-start(f32[1024]{0:T(1024)} %param.11) | copy-start | bytes 12292
  9107.9 2339.7 %all-reduce.3.cloned.1.call-start = ((), (), s32[]{:S(2)}) async-start(), calls=%async_computation.1 | async-start | bytes 16777216 | tf_op jit(solution)/shard_map/psum | solution.py:38
  11254.2 0.7 copy-start.3
  11254.2 0.7 copy-start.6
  11254.3 1243.2 %reduce-scatter.2.cloned.1.call-start = ((), (), s32[]{:S(2)}) async-start(), calls=%async_computation.2 | async-start | bytes 226492416 | tf_op jit(solution)/shard_map/reduce_scatter | solution.py:40
Sparse Core Ops, SparseCore 0:
  9108.1 70.5 sort.4.cloned.1.call-done
  11254.4 193.2 all-reduce.2
  11451.8 1045.6 reduce-scatter.1
  (1 shorter events, 0.0 us)
where the time goes:
time: 12700 us; the launch traced here: 12500 us
  local copies, waits for them, and re-layouts  5190 us (41%)
  blocking collectives  3900 us (31%)
  other arithmetic  1950 us (15%)
  waiting for transfers between devices  1090 us (9%)
  matrix products  349 us (3%)
    gather x3, local copies, waits for them, and re-layouts, local_head(): picked = jnp.take_along_axis(logits, safe_ids, axis=1)  5060 us
    psum x1, blocking collectives, local_head(): lax.psum(jnp.stack([jnp.sum(shifted, axis=1), teach_part], axis=1), 'tp')  3860 us
    unnamed x7, other arithmetic  1860 us
    reduce_scatter x1, waiting for transfers between devices, local_head(): lax.psum_scatter(embed_part, 'dp', scatter_dimension=1, tiled=True)  1020 us
  transfers between devices with their start and end apart: 2, of which 2 were waited for; matrix products, arithmetic and copies ran while one was open for 1% of the time, Pallas kernels for 0%

commit v1 on v0

v1 whole, which is shorter than its diff:
```python
import functools

import jax
import jax.numpy as jnp
from jax import lax
from jax.experimental import pallas as pl
from jax.experimental.pallas import tpu as pltpu
from jax.sharding import PartitionSpec as P

EPS_NORM = 1e-6
LANES = 128
NT = (((1,), (1,)), ((), ()))
TN = (((0,), (0,)), ((), ()))
ORDER = (7, 5, 3, 1, 6, 4, 2, 0)


def flip(value, bit):
    return lax.ppermute(value, 'dp', [(i, i ^ bit) for i in range(8)])


def logits_body(start_ref, u_ref, e_ref, z_ref, m_ref, l_ref):
    rows, width = z_ref.shape

    @pl.when(pl.program_id(0) == 0)
    def _():
        m_ref[...] = jnp.full(m_ref.shape, -jnp.inf, jnp.float32)
        l_ref[...] = jnp.zeros(l_ref.shape, jnp.float32)

    z_ref[...] = lax.dot_general(u_ref[...], e_ref[...], NT, preferred_element_type=jnp.float32)

    def step(i, carry):
        at = pl.ds(pl.multiple_of(i * 32, 32), 32)
        parts = [z_ref[at, c * LANES:(c + 1) * LANES] for c in range(width // LANES)]
        old = m_ref[at, :]
        top = functools.reduce(jnp.maximum, parts, old)
        total = l_ref[at, :] * jnp.exp(old - top)
        for part in parts:
            total = total + jnp.exp(part - top)
        m_ref[at, :] = top
        l_ref[at, :] = total
        return carry

    lax.fori_loop(0, rows // 32, step, 0)


def logits_alias_body(start_ref, u_ref, e_ref, old_ref, z_ref, m_ref, l_ref):
    logits_body(start_ref, u_ref, e_ref, z_ref, m_ref, l_ref)


def logits_call(start, u, e, half, z_old, width, tile):
    rows, depth = u.shape
    in_specs = [
        pl.BlockSpec((rows, depth), lambda j, s: (0, 0)),
        pl.BlockSpec((tile, depth), lambda j, s: (s[0] + j, 0)),
    ]
    operands = [start, u, e]
    aliases = {}
    if z_old is not None:
        in_specs.append(pl.BlockSpec(memory_space=pl.ANY))
        operands.append(z_old)
        aliases = {3: 0}
    stat = pl.BlockSpec((rows, LANES), lambda j, s: (0, 0))
    return pl.pallas_call(
        logits_body if z_old is None else logits_alias_body,
        grid_spec=pltpu.PrefetchScalarGridSpec(
            num_scalar_prefetch=1,
            grid=(width // tile,),
            in_specs=in_specs,
            out_specs=[pl.BlockSpec((rows, tile), lambda j, s: (half, j)), stat, stat],
        ),
        out_shape=[
            jax.ShapeDtypeStruct((2 * rows, width), jnp.float32),
            jax.ShapeDtypeStruct((rows, LANES), jnp.float32),
            jax.ShapeDtypeStruct((rows, LANES), jnp.float32),
        ],
        input_output_aliases=aliases,
        compiler_params=pltpu.CompilerParams(dimension_semantics=('arbitrary',), vmem_limit_bytes=50 * 2 ** 20),
        cost_estimate=pl.CostEstimate(flops=2 * rows * width * depth, bytes_accessed=width * depth * 2 + rows * width * 4, transcendentals=rows * width),
    )(*operands)


PLAN = (
    'g0', 'c0', 'g1', 'y0', 'c1', 'o0', 'y1', 'g2', 'c2', 'o1', 'y2', 's0', 'c3', 'o2', 'y3',
    'g3', 's1', 'p0', 'p1', 'c4', 'o3', 'y4', 'd0', 's2', 'c5', 'o4', 'y5', 'd1', 's3', 'c6',
    'o5', 'y6', 'c7', 'o6', 'y7', 'o7', 's4', 's5', 's6', 's7',
)


GROUP = 16
PITCH = 104


def teach_body(hi_ref, lo_ref, pt_ref, out_ref, scr_ref):
    tokens, width = out_ref.shape
    count = width // LANES
    top = hi_ref.shape[1]
    hi_iota = lax.broadcasted_iota(jnp.int32, (count, top), 0)
    lo_iota = lax.broadcasted_iota(jnp.int32, (LANES, top), 0)

    def step(i, carry):
        for sub in range(GROUP // 8):
            row = pl.multiple_of(i * GROUP + sub * 8, 8)
            hi8 = hi_ref[pl.ds(row, 8), :]
            lo8 = lo_ref[pl.ds(row, 8), :]
            rest = pt_ref[pl.ds(row, 8), :]
            one = rest.astype(jnp.bfloat16).astype(jnp.float32)
            rest = rest - one
            two = rest.astype(jnp.bfloat16).astype(jnp.float32)
            three = rest - two
            for t in range(8):
                hit = hi8[t:t + 1, :] == hi_iota
                left = jnp.concatenate([jnp.where(hit, piece[t:t + 1, :], 0.0).astype(jnp.bfloat16) for piece in (one, two, three)], axis=0)
                right = jnp.where(lo8[t:t + 1, :] == lo_iota, 1.0, 0.0).astype(jnp.bfloat16)
                dense = lax.dot_general(left, right, NT, preferred_element_type=jnp.float32)
                scr_ref[pl.ds((sub * 8 + t) * PITCH, count), :] = dense[:count] + dense[count:2 * count] + dense[2 * count:]
        for sub in range(GROUP // 8):
            row = pl.multiple_of(i * GROUP + sub * 8, 8)
            for h in range(count):
                out_ref[pl.ds(row, 8), h * LANES:(h + 1) * LANES] = scr_ref[pl.ds(sub * 8 * PITCH + h, 8, stride=PITCH), :]
        return carry

    lax.fori_loop(0, tokens // GROUP, step, 0)


def teach_alias_body(hi_ref, lo_ref, pt_ref, old_ref, out_ref, scr_ref):
    teach_body(hi_ref, lo_ref, pt_ref, out_ref, scr_ref)


def teach_call(hi, lo, pt, half, old, width, block):
    rows, top = hi.shape
    steps = rows // block
    spec = pl.BlockSpec((block, top), lambda i: (i, 0))
    in_specs, operands, aliases = [spec] * 3, [hi, lo, pt], {}
    if old is not None:
        in_specs.append(pl.BlockSpec(memory_space=pl.ANY))
        operands.append(old)
        aliases = {3: 0}
    return pl.pallas_call(
        teach_body if old is None else teach_alias_body,
        grid=(steps,),
        in_specs=in_specs,
        out_specs=pl.BlockSpec((block, width), lambda i: (half * steps + i, 0)),
        out_shape=jax.ShapeDtypeStruct((2 * rows, width), jnp.float32),
        scratch_shapes=[pltpu.VMEM((GROUP * PITCH, LANES), jnp.float32)],
        input_output_aliases=aliases,
        compiler_params=pltpu.CompilerParams(dimension_semantics=('arbitrary',), vmem_limit_bytes=40 * 2 ** 20),
        cost_estimate=pl.CostEstimate(flops=6 * rows * width * top, bytes_accessed=rows * width * 4, transcendentals=0),
    )(*operands)


def grad_body(z_ref, p_ref, lz_ref, w_ref, g_ref, t_ref):
    rows, width = z_ref.shape

    @pl.when((pl.program_id(0) == 0) & (pl.program_id(1) == 0))
    def _():
        t_ref[...] = jnp.zeros(t_ref.shape, jnp.float32)

    def step(i, acc):
        at = pl.ds(pl.multiple_of(i * 32, 32), 32)
        lz = lz_ref[at, :]
        w = w_ref[at, :]
        for c in range(width // LANES):
            cols = slice(c * LANES, (c + 1) * LANES)
            z = z_ref[at, cols]
            wp = p_ref[at, cols] * w
            g_ref[at, cols] = (jnp.exp(z - lz) * w - wp).astype(jnp.bfloat16)
            acc = acc + wp * z
        return acc

    acc = lax.fori_loop(0, rows // 32, step, jnp.zeros((32, LANES), jnp.float32))
    t_ref[...] += acc


def grad_call(z, p, log_norm, weight, first, width, rows, tile):
    total = z.shape[0]
    base = first // tile
    wide = pl.BlockSpec((rows, tile), lambda i, j: (i, base + j))
    stat = pl.BlockSpec((rows, LANES), lambda i, j: (i, 0))
    return pl.pallas_call(
        grad_body,
        grid=(total // rows, width // tile),
        in_specs=[wide, wide, stat, stat],
        out_specs=[pl.BlockSpec((rows, tile), lambda i, j: (i, j)), pl.BlockSpec((32, LANES), lambda i, j: (0, 0))],
        out_shape=[jax.ShapeDtypeStruct((total, width), jnp.bfloat16), jax.ShapeDtypeStruct((32, LANES), jnp.float32)],
        compiler_params=pltpu.CompilerParams(dimension_semantics=('arbitrary', 'arbitrary'), vmem_limit_bytes=40 * 2 ** 20),
        cost_estimate=pl.CostEstimate(flops=100 * total * width, bytes_accessed=total * width * 10, transcendentals=total * width),
    )(z, p, log_norm, weight)


def solution(mesh):
    def local_head(hidden, embedding, norm_weight, teach_ids, teach_prob, tok_mask):
        quarter = embedding.shape[0] // 2
        tok, depth = hidden.shape
        block = depth // 8
        dp, tp = lax.axis_index('dp'), lax.axis_index('tp')
        side = (dp >> 1) & 1
        base = tp * embedding.shape[0] + side * quarter

        scale_w = 1.0 + norm_weight
        h_f32 = hidden.astype(jnp.float32)
        inv_rms = lax.rsqrt(jnp.mean(h_f32 * h_f32, axis=1, keepdims=True) + EPS_NORM)
        normed = h_f32 * inv_rms
        mask_total = lax.psum(jnp.sum(tok_mask), 'dp')
        half = tok // 2

        def swap_z(value):
            return lax.ppermute(value, 'tp', [(0, 1), (1, 0)])

        def both_halves(near, far):
            first, second = jnp.where(tp == 0, near, far), jnp.where(tp == 0, far, near)
            return jnp.concatenate([first, second], axis=0)

        mask_pair = flip(tok_mask, 2)
        x_ids = flip(lax.dynamic_slice_in_dim(teach_ids, tp * half, half), 2)
        x_prob = flip(lax.dynamic_slice_in_dim(teach_prob, tp * half, half), 2)
        x_act = [flip(lax.dynamic_slice_in_dim(normed, tp * half + c * (half // 2), half // 2), 2) for c in range(2)]
        z_ids, z_prob = swap_z(x_ids), swap_z(x_prob)
        z_act = [swap_z(x_act[c]) for c in range(2)]
        normed_pair = both_halves(jnp.concatenate(x_act, axis=0), jnp.concatenate(z_act, axis=0))
        u_own = (normed * scale_w).astype(jnp.bfloat16)
        u_pair = (normed_pair * scale_w).astype(jnp.bfloat16)

        def split_ids(ids):
            near = ids - base
            ok = (near >= 0) & (near < quarter)
            return jnp.where(ok, near >> 7, -1), near & (LANES - 1)

        tile = 1024
        start = (side * (quarter // tile)).reshape(1).astype(jnp.int32)
        z, max_own, sum_own = logits_call(start, u_own, embedding, 0, None, quarter, tile)
        first_ids, _ = lax.optimization_barrier((teach_ids, max_own))
        dense = teach_call(*split_ids(first_ids), teach_prob, 0, None, quarter, min(64, tok))
        x_ids, x_prob, z_ids, z_prob, dense = lax.optimization_barrier((x_ids, x_prob, z_ids, z_prob, dense))
        ids_pair, prob_pair = both_halves(x_ids, z_ids), both_halves(x_prob, z_prob)
        dense = teach_call(*split_ids(ids_pair), prob_pair, 1, dense, quarter, min(64, tok))
        u_pair, dense, z = lax.optimization_barrier((u_pair, dense, z))
        z, max_pair, sum_pair = logits_call(start, u_pair, embedding, 1, z, quarter, tile)

        def lane_merge(top, total):
            best = jnp.max(top, axis=1)
            return best, jnp.sum(total * jnp.exp(top - best[:, None]), axis=1)

        own, pair = jnp.stack(lane_merge(max_own, sum_own)), jnp.stack(lane_merge(max_pair, sum_pair))
        stats = jnp.concatenate([own, pair], axis=1)
        swapped = jnp.concatenate([pair, own], axis=1)
        both = [(i, (i ^ 2) ^ 8) for i in range(16)]
        shards = [stats, flip(swapped, 2), lax.ppermute(stats, 'tp', [(0, 1), (1, 0)]), lax.ppermute(swapped, ('tp', 'dp'), both)]
        best = functools.reduce(jnp.maximum, [s[0] for s in shards])
        log_norm = best + jnp.log(sum(s[1] * jnp.exp(s[0] - best) for s in shards))
        weight = jnp.concatenate([tok_mask, mask_pair]) / mask_total
        lz_wide = jnp.broadcast_to(log_norm[:, None], (2 * tok, LANES))
        w_wide = jnp.broadcast_to(weight[:, None], (2 * tok, LANES))

        size = quarter // 8
        u_all = jnp.concatenate([u_own, u_pair], axis=0)
        u_parts = [
            jnp.concatenate([lax.dynamic_slice(u_all, (0, (dp ^ r) * block), (2 * tok, block)) for r in group], axis=1)
            for group in (ORDER[:4], ORDER[4:6], ORDER[6:])
        ]

        last = [log_norm]

        def after(value):
            return lax.optimization_barrier((value, last[0]))[0]

        def mark(value):
            last[0] = value
            return value

        pieces = ((0, 1), (1, 1), (2, 2), (4, 4))
        grads, scores = {}, []
        core, half_y, half_o = {}, {}, {}

        def grad_step(k):
            first, count = pieces[k]
            g, score = grad_call(z, dense, after(lz_wide), w_wide, first * size, count * size, min(512, 2 * tok), 1536)
            mark(score)
            scores.append(score)
            for j in range(first, first + count):
                grads[j] = g[:, (j - first) * size:(j - first + 1) * size]
            grads['piece', k] = g

        def embed_dot(j, k):
            return lax.dot_general(grads[j], after(u_parts[k]), TN, preferred_element_type=jnp.float32)

        def core_step(j):
            core[j] = flip(mark(embed_dot(j, 0)), 1)

        def y_step(j):
            half_y[j] = flip(mark(embed_dot(j, 1) + core[j][:, :2 * block]), 4)

        def own_step(j):
            half_o[j] = mark(embed_dot(j, 2) + core[j][:, 2 * block:])

        x_rows = {}
        grad_embed = [jnp.zeros((2 * quarter, block), jnp.float32)]

        def place(rows, row):
            grad_embed[0] = lax.dynamic_update_slice(grad_embed[0], rows, (row, 0))

        def place_x(j):
            rows, grad_embed[0] = lax.optimization_barrier((x_rows[j], grad_embed[0]))
            place(rows, (1 - side) * quarter + j * size)

        def sum_step(j):
            own, from_y = lax.optimization_barrier((after(half_o[j]), half_y[j]))
            x_rows[j] = flip(own[:, :block] + from_y[:, :block], 2)
            place(mark(own[:, block:] + from_y[:, block:]), side * quarter + j * size)
            if j >= 3:
                place_x(j - 3)

        half_depth = depth // 2
        from_x, grad_half = {}, {}

        def du_dot(row, col):
            total = None
            for k, (first, count) in enumerate(pieces):
                e = lax.dynamic_slice(embedding, (side * quarter + first * size, col), (count * size, half_depth))
                g = grads['piece', k][row:row + tok]
                term = jnp.dot(after(g) if k == 0 else g, e, preferred_element_type=jnp.float32)
                total = term if total is None else total + term
            return total

        def pair_step(i):
            from_x[i] = flip(mark(du_dot(tok, i * half_depth)), 2)

        def du_step(i):
            total = mark(du_dot(0, i * half_depth) + from_x[i])
            other = lax.ppermute(total, 'tp', [(0, 1), (1, 0)])
            grad_half[i] = total + other

        steps = {'g': grad_step, 'c': core_step, 'y': y_step, 'o': own_step, 's': sum_step, 'p': pair_step, 'd': du_step}
        for word in PLAN:
            steps[word[0]](int(word[1:]))
        for j in range(5, 8):
            place_x(j)
        grad_embed = grad_embed[0]

        grad_u = jnp.concatenate([grad_half[0], grad_half[1]], axis=1)
        d_normed = grad_u * scale_w
        grad_hidden = (inv_rms * (d_normed - normed * jnp.mean(d_normed * normed, axis=1, keepdims=True))).astype(jnp.bfloat16)
        grad_norm = lax.psum(jnp.sum(grad_u * normed, axis=0), 'dp')
        score = sum(jnp.sum(part) for part in scores) - 0.5 * jnp.sum(weight[:tok] * log_norm[:tok])
        loss_mean = -lax.psum(score, ('tp', 'dp'))
        return loss_mean, grad_hidden, grad_embed, grad_norm

    return jax.shard_map(local_head, mesh=mesh, in_specs=(P('dp', None), P('tp', None), P(None), P('dp', None), P('dp', None), P('dp')), out_specs=(P(), P('dp', None), P('tp', 'dp'), P(None)), check_vma=False)
```

time: 12700 us -> 1640 us (0.13); the launches traced: 12500 us -> 1640 us
  local copies, waits for them, and re-layouts: 5190 us -> 43.2 us
  blocking collectives: 3900 us -> 289 us
  other arithmetic: 1950 us -> 67.7 us
  waiting for transfers between devices: 1090 us -> 446 us
  Pallas kernels: 0 us -> 354 us
    gather x3 -> x0, local copies, waits for them, and re-layouts: 5060 us -> none  [local_head(): picked = jnp.take_along_axis(logits, safe_ids, axis=1)]
    psum x2, blocking collectives: 3880 us -> 276 us  [the longest x1 200 us: local_head(): loss_mean = -lax.psum(score, ('tp', 'dp'))]
    unnamed x7 -> x3, other arithmetic: 1860 us -> 0.01 us
    reduce_scatter x1 -> x0, waiting for transfers between devices: 1020 us -> none  [local_head(): lax.psum_scatter(embed_part, 'dp', scatter_dimension=1, tiled=True)]
    ppermute x0 -> x40, waiting for transfers between devices: none -> 446 us  [the longest x32 417 us: flip(): return lax.ppermute(value, 'dp', [(i, i ^ bit) for i in range(8)])]
    pallas_call x0 -> x8, Pallas kernels: none -> 354 us  [the longest x2 152 us: logits_call(): pl.pallas_call(logits_body if z_old is None else logits_alias_body, grid_...]
    dot_general x3 -> x40, matrix products: 349 us -> 391 us  [the longest x24 203 us: embed_dot(): lax.dot_general(grads[j], after(u_parts[k]), TN, preferred_element_type=j...]
  transfers between devices with their start and end apart: 2 -> 40, of which waited for: 2 -> 12; matrix products, arithmetic and copies ran while one was open for 1% -> 19% of each run, Pallas kernels for 0% -> 15%
where the time goes in v1:
time: 1640 us
  waiting for transfers between devices  446 us (27%)
  matrix products  391 us (24%)
  Pallas kernels  354 us (22%)
  blocking collectives  289 us (18%)
  other arithmetic  67.7 us (4%)
  local copies, waits for them, and re-layouts  43.2 us (3%)
  starting transfers between devices  37.2 us (2%)
    ppermute x32, waiting for transfers between devices, flip(): return lax.ppermute(value, 'dp', [(i, i ^ bit) for i in range(8)])  417 us
    dot_general x24, matrix products, embed_dot(): lax.dot_general(grads[j], after(u_parts[k]), TN, preferred_element_type=j...  203 us
    psum x1, blocking collectives, local_head(): loss_mean = -lax.psum(score, ('tp', 'dp'))  200 us
    dot_general x16, matrix products, du_dot(): jnp.dot(after(g) if k == 0 else g, e, preferred_element_type=jnp.float32)  188 us
    pallas_call x2, Pallas kernels, logits_call(): pl.pallas_call(logits_body if z_old is None else logits_alias_body, grid_...  152 us
    pallas_call x2, Pallas kernels, teach_call(): pl.pallas_call(teach_body if old is None else teach_alias_body, grid=(ste...  114 us
    pallas_call x4, Pallas kernels, grad_call(): pl.pallas_call(grad_body, grid=(total // rows, width // tile), in_specs=[...  88.1 us
    psum x1, blocking collectives, local_head(): grad_norm = lax.psum(jnp.sum(grad_u * normed, axis=0), 'dp')  76.1 us
  transfers between devices with their start and end apart: 40, of which 12 were waited for; matrix products, arithmetic and copies ran while one was open for 19% of the time, Pallas kernels for 15%

profile of v1, /device:TPU:0, one launch (start us, length us, event | category | flops | bytes accessed | tf_op | source)
XLA Modules:
  0.0 1635.6 jit_solution(12596453080291178420)
XLA Ops:
  26.3 76.0 %shard_map.93 = (f32[2048,12288]{1,0:T(8,128)}, f32[1024,128]{1,0:T(8,128)S(1)}, f32[1024,128]{1,0:T(8,128)S(1)}) custom-call(s32[1]{0:T(128)} %bitcast.start_ref, bf16[1024,2048]{1,0:T(8,128)(2,1)} %get-tuple-element.233.u_ref, bf16[24576,2048]{1,0:T(8,128)(2,1)} %e_ref.3), custom_call_target="tpu_custom_call" | custom-call | flops 51539607552 | bytes 100663296 | tf_op jit(solution)/shard_map/pallas_call | solution.py:63
  102.5 21.0 %collective-permute-done.4 = s32[512,256]{1,0:T(8,128)} collective-permute-done((s32[512,256]{1,0:T(8,128)}, s32[512,256]{1,0:T(8,128)}, u32[]{:S(2)}, u32[]{:S(2)}) %collective-permute-start.4) | collective-permute-done | bytes 524320 | tf_op jit(solution)/shard_map/ppermute | solution.py:18
  135.8 57.0 %shard_map.94.old_ref = f32[2048,12288]{1,0:T(8,128)} custom-call(s32[1024,256]{1,0:T(8,128)S(1)} %get-tuple-element.242.hi_ref, s32[1024,256]{1,0:T(8,128)S(1)} %get-tuple-element.241.lo_ref, f32[1024,256]{1,0:T(8,128)S(1)} %copy-done.1), custom_call_target="tpu_custom_call" | custom-call | flops 19327352832 | bytes 50331648 | tf_op jit(solution)/shard_map/pallas_call | solution.py:138
  194.0 13.3 psum.21
  212.7 57.0 %shard_map.95.p_ref = f32[2048,12288]{1,0:T(8,128)} custom-call(s32[1024,256]{1,0:T(8,128)S(1)} %get-tuple-element.238.hi_ref, s32[1024,256]{1,0:T(8,128)S(1)} %get-tuple-element.237.lo_ref, f32[1024,256]{1,0:T(8,128)S(1)} %pad_maximum_fusion.4.pt_ref, f32[2048,12288]{1,0:T(8,128)} %shard_map.94.old_ref), custom_call_target="tpu_custom_call", output_to_operand_aliasing={{}: (3, {})} | custom-call | flops 19327352832 | bytes 50331648 | tf_op jit(solution)/shard_map/pallas_call | solution.py:138
  273.3 29.2 %collective-permute-done.3 = f32[256,2048]{1,0:T(8,128)S(1)} collective-permute-done((f32[256,2048]{1,0:T(8,128)}, f32[256,2048]{1,0:T(8,128)S(1)}, u32[]{:S(2)}, u32[]{:S(2)}) %collective-permute-start.3) | collective-permute-done | bytes 2097184 | tf_op jit(solution)/shard_map/ppermute | solution.py:207
  307.0 76.0 %shard_map.96 = (f32[2048,12288]{1,0:T(8,128)}, f32[1024,128]{1,0:T(8,128)S(1)}, f32[1024,128]{1,0:T(8,128)S(1)}) custom-call(s32[1]{0:T(128)} %bitcast.start_ref, bf16[1024,2048]{1,0:T(8,128)(2,1)} %fusion.13.u_ref, bf16[24576,2048]{1,0:T(8,128)(2,1)} %e_ref.3, f32[2048,12288]{1,0:T(8,128)} %get-tuple-element.108.old_ref), custom_call_target="tpu_custom_call", output_to_operand_aliasing={{0}: (3, {})} | custom-call | flops 51539607552 | bytes 100663296 | tf_op jit(solution)/shard_map/pallas_call | solution.py:63
  459.2 22.6 %shard_map.99 = (bf16[2048,3072]{1,0:T(8,128)(2,1)}, f32[32,128]{1,0:T(8,128)S(1)}) custom-call(f32[2048,12288]{1,0:T(8,128)} %get-tuple-element.109.z_ref, f32[2048,12288]{1,0:T(8,128)} %shard_map.95.p_ref, f32[2048,128]{1,0:T(8,128)S(1)} %broadcast_in_dim.12.lz_ref, f32[2048,128]{1,0:T(8,128)S(1)} %broadcast_in_dim.13.w_ref), custom_call_target="tpu_custom_call" | custom-call | flops 629145600 | bytes 62914560 | tf_op jit(solution)/shard_map/pallas_call | solution.py:179
  510.2 53.0 %collective-permute-done.15 = f32[1536,512]{1,0:T(8,128)} collective-permute-done((f32[1536,512]{1,0:T(8,128)}, f32[1536,512]{1,0:T(8,128)}, u32[]{:S(2)}, u32[]{:S(2)}) %collective-permute-start.15) | collective-permute-done | bytes 3145760 | tf_op jit(solution)/shard_map/ppermute | solution.py:18
  637.3 43.5 %shard_map.100 = (bf16[2048,6144]{1,0:T(8,128)(2,1)}, f32[32,128]{1,0:T(8,128)S(1)}) custom-call(f32[2048,12288]{1,0:T(8,128)} %get-tuple-element.109.z_ref, f32[2048,12288]{1,0:T(8,128)} %shard_map.95.p_ref, f32[2048,128]{1,0:T(8,128)S(1)} %broadcast_in_dim.12.lz_ref, f32[2048,128]{1,0:T(8,128)S(1)} %broadcast_in_dim.13.w_ref), custom_call_target="tpu_custom_call" | custom-call | flops 1258291200 | bytes 125829120 | tf_op jit(solution)/shard_map/pallas_call | solution.py:179
  680.8 19.1 %fusion.4 = f32[1024,1024]{1,0:T(8,128)} fusion(bf16[2048,6144]{1,0:T(8,128)(2,1)} %get-tuple-element.139, bf16[24576,2048]{1,0:T(8,128)(2,1)} %e_ref.3, s32[]{:T(128)S(6)} %select_n.160), kind=kOutput, calls=%fused_computation.20 | convolution fusion | flops 12884901888 | bytes 29360132 | tf_op jit(solution)/shard_map/dot_general | solution.py:320
  699.8 19.2 %fusion.6 = f32[1024,1024]{1,0:T(8,128)} fusion(bf16[2048,6144]{1,0:T(8,128)(2,1)} %get-tuple-element.139, bf16[24576,2048]{1,0:T(8,128)(2,1)} %e_ref.3, s32[]{:T(128)S(6)} %select_n.160), kind=kOutput, calls=%fused_computation.22 | convolution fusion | flops 12884901888 | bytes 29360132 | tf_op jit(solution)/shard_map/dot_general | solution.py:320
  726.6 13.0 add_add_fusion.3
  745.2 12.9 add_add_fusion.2
  782.1 19.3 %fusion.2 = f32[1024,1024]{1,0:T(8,128)} fusion(bf16[2048,6144]{1,0:T(8,128)(2,1)} %get-tuple-element.139, bf16[24576,2048]{1,0:T(8,128)(2,1)} %e_ref.3, s32[]{:T(128)S(6)} %select_n.160), kind=kOutput, calls=%fused_computation.18 | convolution fusion | flops 12884901888 | bytes 29360132 | tf_op jit(solution)/shard_map/dot_general | solution.py:320
  817.3 57.2 %collective-permute-done.19 = f32[1024,1024]{1,0:T(8,128)} collective-permute-done((f32[1024,1024]{1,0:T(8,128)}, f32[1024,1024]{1,0:T(8,128)}, u32[]{:S(2)}, u32[]{:S(2)}) %collective-permute-start.19) | collective-permute-done | bytes 4194336 | tf_op jit(solution)/shard_map/ppermute | solution.py:18
  911.3 19.0 %fusion = f32[1024,1024]{1,0:T(8,128)} fusion(bf16[2048,6144]{1,0:T(8,128)(2,1)} %get-tuple-element.139, bf16[24576,2048]{1,0:T(8,128)(2,1)} %e_ref.3, s32[]{:T(128)S(6)} %select_n.160), kind=kOutput, calls=%fused_computation.16 | convolution fusion | flops 12884901888 | bytes 29360132 | tf_op jit(solution)/shard_map/dot_general | solution.py:320
  946.0 57.1 %collective-permute-done.23 = f32[1024,1024]{1,0:T(8,128)} collective-permute-done((f32[1024,1024]{1,0:T(8,128)}, f32[1024,1024]{1,0:T(8,128)}, u32[]{:S(2)}, u32[]{:S(2)}) %collective-permute-start.23) | collective-permute-done | bytes 4194336 | tf_op jit(solution)/shard_map/ppermute | solution.py:18
  1064.5 199.8 %psum.22 = f32[]{:T(128)} all-reduce(f32[]{:T(128)S(6)} %sub.81), channel_id=1, replica_groups=mesh['tp'=2,'dp'=8] {'tp','dp'}, use_global_device_ids=true, to_apply=%region_12.13 | all-reduce | flops 1 | bytes 8 | tf_op jit(solution)/shard_map/psum | solution.py:344
  1309.0 29.4 %collective-permute-done.28 = f32[1536,512]{1,0:T(8,128)S(1)} collective-permute-done((f32[1536,512]{1,0:T(8,128)}, f32[1536,512]{1,0:T(8,128)S(1)}, u32[]{:S(2)}, u32[]{:S(2)}) %collective-permute-start.28) | collective-permute-done | bytes 3145760 | tf_op jit(solution)/shard_map/ppermute | solution.py:18
  1342.7 63.2 %collective-permute-done.29 = f32[1536,512]{1,0:T(8,128)S(1)} collective-permute-done((f32[1536,512]{1,0:T(8,128)S(1)}, f32[1536,512]{1,0:T(8,128)S(1)}, u32[]{:S(2)}, u32[]{:S(2)}) %collective-permute-start.29) | collective-permute-done | bytes 3145760 | tf_op jit(solution)/shard_map/ppermute | solution.py:18
  1408.7 64.6 %collective-permute-done.30 = f32[1536,512]{1,0:T(8,128)S(1)} collective-permute-done((f32[1536,512]{1,0:T(8,128)}, f32[1536,512]{1,0:T(8,128)S(1)}, u32[]{:S(2)}, u32[]{:S(2)}) %collective-permute-start.30) | collective-permute-done | bytes 3145760 | tf_op jit(solution)/shard_map/ppermute | solution.py:18
  1479.4 58.3 %collective-permute-done.31 = f32[1536,512]{1,0:T(8,128)S(1)} collective-permute-done((f32[1536,512]{1,0:T(8,128)}, f32[1536,512]{1,0:T(8,128)S(1)}, u32[]{:S(2)}, u32[]{:S(2)}) %collective-permute-start.31) | collective-permute-done | bytes 3145760 | tf_op jit(solution)/shard_map/ppermute | solution.py:18
  1540.3 76.1 %psum.23 = f32[2048]{0:T(1024)} all-reduce(f32[2048]{0:T(1024)S(1)} %get-tuple-element.194), channel_id=1, replica_groups=mesh['tp'=2,'dp'=8] {'dp'}, use_global_device_ids=true, to_apply=%region_15.16 | all-reduce | flops 2048 | bytes 16384 | tf_op jit(solution)/shard_map/psum | solution.py:342
  (281 shorter events, 471.8 us)
Async XLA Ops:
  17.4 193.2 %collective-permute-start = (f32[256,2048]{1,0:T(8,128)}, f32[256,2048]{1,0:T(8,128)}, u32[]{:S(2)}, u32[]{:S(2)}) collective-permute-start(f32[256,2048]{1,0:T(8,128)} %get-tuple-element.221), channel_id=1, source_target_pairs={{0,2},{1,3},{2,0},{3,1},{4,6},{5,7},{6,4},{7,5},{8,10},{9,11},{10,... | collective-permute-start | bytes 6291464 | tf_op jit(solution)/shard_map/ppermute | solution.py:18
  20.6 190.5 %collective-permute-start.1 = (f32[256,2048]{1,0:T(8,128)}, f32[256,2048]{1,0:T(8,128)}, u32[]{:S(2)}, u32[]{:S(2)}) collective-permute-start(f32[256,2048]{1,0:T(8,128)} %get-tuple-element.220), channel_id=1, source_target_pairs={{0,2},{1,3},{2,0},{3,1},{4,6},{5,7},{6,4},{7,5},{8,10},{9,11},{10,... | collective-permute-start | bytes 6291464 | tf_op jit(solution)/shard_map/ppermute | solution.py:18
  21.4 102.1 %collective-permute-start.4 = (s32[512,256]{1,0:T(8,128)}, s32[512,256]{1,0:T(8,128)}, u32[]{:S(2)}, u32[]{:S(2)}) collective-permute-start(s32[512,256]{1,0:T(8,128)} %constant_dynamic-slice_fusion.1), channel_id=1, source_target_pairs={{0,2},{1,3},{2,0},{3,1},{4,6},{5,7},{6,4},{7,5},{8,10},{9,11},{10,... | collective-permute-start | bytes 1572872 | tf_op jit(solution)/shard_map/ppermute | solution.py:18
  24.2 109.7 %collective-permute-start.5 = (f32[512,256]{1,0:T(8,128)}, f32[512,256]{1,0:T(8,128)}, u32[]{:S(2)}, u32[]{:S(2)}) collective-permute-start(f32[512,256]{1,0:T(8,128)} %constant_dynamic-slice_fusion), channel_id=1, source_target_pairs={{0,2},{1,3},{2,0},{3,1},{4,6},{5,7},{6,4},{7,5},{8,10},{9,11},{10,... | collective-permute-start | bytes 1572872 | tf_op jit(solution)/shard_map/ppermute | solution.py:18
  24.3 183.1 %collective-permute-start.11 = (f32[1024]{0:T(1024)S(1)}, f32[1024]{0:T(1024)S(1)}, u32[]{:S(2)}, u32[]{:S(2)}) collective-permute-start(f32[1024]{0:T(1024)S(1)} %copy-done.38), channel_id=1, source_target_pairs={{0,2},{1,3},{2,0},{3,1},{4,6},{5,7},{6,4},{7,5},{8,10},{9,11},{10,... | collective-permute-start | bytes 12296 | tf_op jit(solution)/shard_map/ppermute | solution.py:18
  123.5 84.5 %collective-permute-start.6 = (s32[512,256]{1,0:T(8,128)}, s32[512,256]{1,0:T(8,128)S(1)}, u32[]{:S(2)}, u32[]{:S(2)}) collective-permute-start(s32[512,256]{1,0:T(8,128)} %collective-permute-done.4), channel_id=1, source_target_pairs={{0,8},{8,0},{1,9},{9,1},{2,10},{10,2},{3,11},{11,3},{4,12},{12,4},... | collective-permute-start | bytes 1572872 | tf_op jit(solution)/shard_map/ppermute | solution.py:207
  211.1 91.4 %collective-permute-start.3 = (f32[256,2048]{1,0:T(8,128)}, f32[256,2048]{1,0:T(8,128)S(1)}, u32[]{:S(2)}, u32[]{:S(2)}) collective-permute-start(f32[256,2048]{1,0:T(8,128)} %collective-permute-done.1), channel_id=1, source_target_pairs={{0,8},{8,0},{1,9},{9,1},{2,10},{10,2},{3,11},{11,3},{4,12},{12,4},... | collective-permute-start | bytes 6291464 | tf_op jit(solution)/shard_map/ppermute | solution.py:207
  618.9 100.1 %collective-permute-start.17 = (f32[1536,512]{1,0:T(8,128)S(1)}, f32[1536,512]{1,0:T(8,128)S(1)}, u32[]{:S(2)}, u32[]{:S(2)}) collective-permute-start(f32[1536,512]{1,0:T(8,128)S(1)} %copy-done.44), channel_id=1, source_target_pairs={{0,4},{1,5},{2,6},{3,7},{4,0},{5,1},{6,2},{7,3},{8,12},{9,13},{10,... | collective-permute-start | bytes 9437192 | tf_op jit(solution)/shard_map/ppermute | solution.py:18
  781.1 103.7 %collective-permute-start.21 = (f32[1536,512]{1,0:T(8,128)S(1)}, f32[1536,512]{1,0:T(8,128)S(1)}, u32[]{:S(2)}, u32[]{:S(2)}) collective-permute-start(f32[1536,512]{1,0:T(8,128)S(1)} %copy-done.43), channel_id=1, source_target_pairs={{0,4},{1,5},{2,6},{3,7},{4,0},{5,1},{6,2},{7,3},{8,12},{9,13},{10,... | collective-permute-start | bytes 9437192 | tf_op jit(solution)/shard_map/ppermute | solution.py:18
  782.1 92.4 %collective-permute-start.19 = (f32[1024,1024]{1,0:T(8,128)}, f32[1024,1024]{1,0:T(8,128)}, u32[]{:S(2)}, u32[]{:S(2)}) collective-permute-start(f32[1024,1024]{1,0:T(8,128)} %add_add_fusion.3), channel_id=1, source_target_pairs={{0,2},{1,3},{2,0},{3,1},{4,6},{5,7},{6,4},{7,5},{8,10},{9,11},{10,... | collective-permute-start | bytes 12582920 | tf_op jit(solution)/shard_map/ppermute | solution.py:18
  909.8 93.3 %collective-permute-start.23 = (f32[1024,1024]{1,0:T(8,128)}, f32[1024,1024]{1,0:T(8,128)}, u32[]{:S(2)}, u32[]{:S(2)}) collective-permute-start(f32[1024,1024]{1,0:T(8,128)} %add_add_fusion.2), channel_id=1, source_target_pairs={{0,2},{1,3},{2,0},{3,1},{4,6},{5,7},{6,4},{7,5},{8,10},{9,11},{10,... | collective-permute-start | bytes 12582920 | tf_op jit(solution)/shard_map/ppermute | solution.py:18
  910.0 103.2 %collective-permute-start.25 = (f32[1536,512]{1,0:T(8,128)}, f32[1536,512]{1,0:T(8,128)S(1)}, u32[]{:S(2)}, u32[]{:S(2)}) collective-permute-start(f32[1536,512]{1,0:T(8,128)} %slice_add_fusion.9), channel_id=1, source_target_pairs={{0,4},{1,5},{2,6},{3,7},{4,0},{5,1},{6,2},{7,3},{8,12},{9,13},{10,... | collective-permute-start | bytes 9437192 | tf_op jit(solution)/shard_map/ppermute | solution.py:18
  1055.6 236.9 %collective-permute-start.27 = (f32[1536,1024]{1,0:T(8,128)}, f32[1536,1024]{1,0:T(8,128)}, u32[]{:S(2)}, u32[]{:S(2)}) collective-permute-start(f32[1536,1024]{1,0:T(8,128)} %fusion.36), channel_id=1, source_target_pairs={{0,1},{1,0},{2,3},{3,2},{4,5},{5,4},{6,7},{7,6},{8,9},{9,8},{10,11... | collective-permute-start | bytes 18874376 | tf_op jit(solution)/shard_map/ppermute | solution.py:18
  1055.8 211.5 %collective-permute-start.20 = (f32[1024,1024]{1,0:T(8,128)}, f32[1024,1024]{1,0:T(8,128)}, u32[]{:S(2)}, u32[]{:S(2)}) collective-permute-start(f32[1024,1024]{1,0:T(8,128)} %add_add_fusion.1), channel_id=1, source_target_pairs={{0,8},{8,0},{1,9},{9,1},{2,10},{10,2},{3,11},{11,3},{4,12},{12,4},... | collective-permute-start | bytes 12582920 | tf_op jit(solution)/shard_map/ppermute | solution.py:329
  1056.2 220.2 %collective-permute-start.24 = (f32[1024,1024]{1,0:T(8,128)}, f32[1024,1024]{1,0:T(8,128)}, u32[]{:S(2)}, u32[]{:S(2)}) collective-permute-start(f32[1024,1024]{1,0:T(8,128)} %add_add_fusion), channel_id=1, source_target_pairs={{0,8},{8,0},{1,9},{9,1},{2,10},{10,2},{3,11},{11,3},{4,12},{12,4},... | collective-permute-start | bytes 12582920 | tf_op jit(solution)/shard_map/ppermute | solution.py:329
  1057.8 214.6 %collective-permute-start.39 = (f32[1536,256]{1,0:T(8,128)}, f32[1536,256]{1,0:T(8,128)}, u32[]{:S(2)}, u32[]{:S(2)}) collective-permute-start(f32[1536,256]{1,0:T(8,128)} %get-tuple-element.228), channel_id=1, source_target_pairs={{0,2},{1,3},{2,0},{3,1},{4,6},{5,7},{6,4},{7,5},{8,10},{9,11},{10,... | collective-permute-start | bytes 4718600 | tf_op jit(solution)/shard_map/ppermute | solution.py:18
  1272.4 133.5 %collective-permute-start.29 = (f32[1536,512]{1,0:T(8,128)S(1)}, f32[1536,512]{1,0:T(8,128)S(1)}, u32[]{:S(2)}, u32[]{:S(2)}) collective-permute-start(f32[1536,512]{1,0:T(8,128)S(1)} %copy-done.42), channel_id=1, source_target_pairs={{0,4},{1,5},{2,6},{3,7},{4,0},{5,1},{6,2},{7,3},{8,12},{9,13},{10,... | collective-permute-start | bytes 9437192 | tf_op jit(solution)/shard_map/ppermute | solution.py:18
  1283.7 189.5 %collective-permute-start.30 = (f32[1536,512]{1,0:T(8,128)}, f32[1536,512]{1,0:T(8,128)S(1)}, u32[]{:S(2)}, u32[]{:S(2)}) collective-permute-start(f32[1536,512]{1,0:T(8,128)} %slice_add_fusion.3), channel_id=1, source_target_pairs={{0,4},{1,5},{2,6},{3,7},{4,0},{5,1},{6,2},{7,3},{8,12},{9,13},{10,... | collective-permute-start | bytes 9437192 | tf_op jit(solution)/shard_map/ppermute | solution.py:18
  1300.9 236.8 %collective-permute-start.31 = (f32[1536,512]{1,0:T(8,128)}, f32[1536,512]{1,0:T(8,128)S(1)}, u32[]{:S(2)}, u32[]{:S(2)}) collective-permute-start(f32[1536,512]{1,0:T(8,128)} %slice_add_fusion.1), channel_id=1, source_target_pairs={{0,4},{1,5},{2,6},{3,7},{4,0},{5,1},{6,2},{7,3},{8,12},{9,13},{10,... | collective-permute-start | bytes 9437192 | tf_op jit(solution)/shard_map/ppermute | solution.py:18
  1340.7 135.4 %collective-permute-start.36 = (f32[1536,256]{1,0:T(8,128)S(1)}, f32[1536,256]{1,0:T(8,128)S(1)}, u32[]{:S(2)}, u32[]{:S(2)}) collective-permute-start(f32[1536,256]{1,0:T(8,128)S(1)} %copy-done.28), channel_id=1, source_target_pairs={{0,2},{1,3},{2,0},{3,1},{4,6},{5,7},{6,4},{7,5},{8,10},{9,11},{10,... | collective-permute-start | bytes 4718600 | tf_op jit(solution)/shard_map/ppermute | solution.py:18
  1476.1 152.7 %collective-permute-start.33 = (f32[1536,256]{1,0:T(8,128)S(1)}, f32[1536,256]{1,0:T(8,128)}, u32[]{:S(2)}, u32[]{:S(2)}) collective-permute-start(f32[1536,256]{1,0:T(8,128)S(1)} %get-tuple-element.227), channel_id=1, source_target_pairs={{0,2},{1,3},{2,0},{3,1},{4,6},{5,7},{6,4},{7,5},{8,10},{9,11},{10,... | collective-permute-start | bytes 4718600 | tf_op jit(solution)/shard_map/ppermute | solution.py:18
  1476.1 149.9 %collective-permute-start.34 = (f32[1536,256]{1,0:T(8,128)S(1)}, f32[1536,256]{1,0:T(8,128)}, u32[]{:S(2)}, u32[]{:S(2)}) collective-permute-start(f32[1536,256]{1,0:T(8,128)S(1)} %get-tuple-element.226), channel_id=1, source_target_pairs={{0,2},{1,3},{2,0},{3,1},{4,6},{5,7},{6,4},{7,5},{8,10},{9,11},{10,... | collective-permute-start | bytes 4718600 | tf_op jit(solution)/shard_map/ppermute | solution.py:18
  1478.1 145.3 %collective-permute-start.35 = (f32[1536,256]{1,0:T(8,128)}, f32[1536,256]{1,0:T(8,128)}, u32[]{:S(2)}, u32[]{:S(2)}) collective-permute-start(f32[1536,256]{1,0:T(8,128)} %get-tuple-element.225), channel_id=1, source_target_pairs={{0,2},{1,3},{2,0},{3,1},{4,6},{5,7},{6,4},{7,5},{8,10},{9,11},{10,... | collective-permute-start | bytes 4718600 | tf_op jit(solution)/shard_map/ppermute | solution.py:18
  1539.8 91.6 %collective-permute-start.32 = (f32[1536,256]{1,0:T(8,128)}, f32[1536,256]{1,0:T(8,128)}, u32[]{:S(2)}, u32[]{:S(2)}) collective-permute-start(f32[1536,256]{1,0:T(8,128)} %get-tuple-element.223), channel_id=1, source_target_pairs={{0,2},{1,3},{2,0},{3,1},{4,6},{5,7},{6,4},{7,5},{8,10},{9,11},{10,... | collective-permute-start | bytes 4718600 | tf_op jit(solution)/shard_map/ppermute | solution.py:18
  (69 other events, 1561.8 us)
